TPU v7x, 128 devices: a whole 4x4x4 slice. The times are simulated.
128 devices in a mesh: row: 8 (over x_lo, z), col: 16 (over x_hi, y, core).
Axes of the slice: x: 4 (x_hi: 2, x_lo: 2; x = x_hi * 2 + x_lo), y: 4, z: 4, core: 2. Of those that a mesh axis runs over, the one named last changes fastest.
Arguments:
- loadings: float32 [64, 32, 16384], P(None, None, ('row', 'col')), may hold values from -6 to 6
Outputs:
- correlation: float32 [16384, 16384], P('row', 'col')
All inputs are finite; a program needn't handle non-finite values.
Results may differ from a plain program's by a relative error of at most 0.000096.
Values sent between devices are 32-bit elements; how exact they have to be, the bound alone decides.
A program may use at most 128 MiB of HBM per device.

v0:
```python
import jax
import jax.numpy as jnp
from jax import lax
from jax.sharding import PartitionSpec as P


def padded_to(lines, devices):
    spare = -len(lines) % devices
    return jnp.pad(lines, [(0, spare)] + [(0, 0)] * (lines.ndim - 1))


def broadcast_by_parts(value, axis, root):
    lines = jnp.where(lax.axis_index(axis) == root, value, jnp.zeros_like(value)).reshape(
        -1, *value.shape[1:][-1:]
    )
    padded = padded_to(lines, lax.axis_size(axis))
    own = lax.psum_scatter(padded, axis, scatter_dimension=0, tiled=True)
    return lax.all_gather(own, axis, axis=0, tiled=True)[: len(lines)].reshape(value.shape)


def tile_product(left, right, count):
    depth = left.shape[0] * left.shape[1]
    flat_left = left.reshape(depth, left.shape[2])
    flat_right = right.reshape(depth, right.shape[2])
    total = lax.dot_general(
        flat_left,
        flat_right,
        (((0,), (0,)), ((), ())),
        precision=lax.Precision.HIGHEST,
        preferred_element_type=jnp.float32,
    )
    return total * (1.0 / count)


def column_source(group_block):
    halves = lax.axis_size("col") // lax.axis_size("row")
    width = group_block.shape[2] // halves
    position = lax.axis_index("col")
    start = position % halves * width
    candidate = lax.dynamic_slice_in_dim(group_block, start, width, 2)
    return broadcast_by_parts(candidate, "row", position // halves)


def local(loadings):
    count = loadings.shape[0]
    variance = jnp.sum(loadings * loadings, axis=1, keepdims=True)
    scaled = loadings / jnp.sqrt(variance)
    group_block = lax.all_gather(scaled, "col", axis=2, tiled=True)
    columns_block = column_source(group_block)
    return tile_product(lax.all_gather(scaled, "col", axis=2, tiled=True), columns_block, count)


def solution(mesh):
    placed = (P(None, None, ("row", "col")),)
    return jax.shard_map(
        local, mesh=mesh, in_specs=placed, out_specs=P("row", "col"), check_vma=False
    )
```

profile of v0, /device:TPU:35, one launch (start us, length us, event | category | flops | bytes accessed | tf_op | source)
XLA Modules:
  0.0 385.2 jit_solution(10311597832348095718)
XLA Ops:
  6.5 0.0 all-gather.3.cloned.1.call-start
  6.5 1.4 multiply_reduce_fusion
  8.0 2.3 broadcast_divide_fusion
  10.3 0.0 all-gather.3.cloned.1.call-update
  10.3 0.0 reduce-scatter.2.cloned.1.call-start
  10.4 119.6 %all-gather.3.cloned.1.call-done = f32[64,32,2048]{2,1,0:T(8,128)} async-done(((f32[64,32,128]{2,1,0:T(8,128)}), f32[64,32,2048]{2,1,0:T(8,128)}) %all-gather.3.cloned.1.call-update) | async-done | bytes 16777232 | tf_op jit(solution)/shard_map/all_gather | solution.py:50
  130.1 8.7 %dynamic-slice_select_fusion = f32[64,32,1024]{2,1,0:T(8,128)} fusion(f32[64,32,2048]{2,1,0:T(8,128)} %all-gather.3.cloned.1.call-done, s32[]{:T(128)S(6)} %select_n.25, pred[]{:T(512)S(6)} %eq.5), kind=kLoop, calls=%fused_computation | loop fusion | flops 2097152 | bytes 16777220 | tf_op jit(solution)/shard_map/jit(_where)/select_n | solution.py:13
  138.7 0.0 reduce-scatter.2.cloned.1.call-update
  138.8 0.0 all-gather.5.cloned.1.call-start
  138.8 88.4 %reduce-scatter.2.cloned.1.call-done = f32[256,1024]{1,0:T(8,128)} async-done(((f32[2048,1024]{1,0:T(8,128)}), f32[256,1024]{1,0:T(8,128)}) %reduce-scatter.2.cloned.1.call-update) | async-done | bytes 1048592 | tf_op jit(solution)/shard_map/reduce_scatter | solution.py:17
  227.2 0.0 all-gather.5.cloned.1.call-update
  227.2 92.3 %all-gather.5.cloned.1.call-done = f32[2048,1024]{1,0:T(8,128)} async-done(((f32[256,1024]{1,0:T(8,128)}), f32[2048,1024]{1,0:T(8,128)}) %all-gather.5.cloned.1.call-update) | async-done | bytes 8388624 | tf_op jit(solution)/shard_map/all_gather | solution.py:18
  319.5 59.2 %convolution_multiply_fusion = f32[2048,1024]{1,0:T(8,128)} fusion(f32[2048,2048]{1,0:T(8,128)} %bitcast.5, f32[2048,1024]{1,0:T(8,128)} %all-gather.5.cloned.1.call-done), kind=kOutput, calls=%fused_computation.1 | convolution fusion | flops 51541704704 | bytes 33554432 | tf_op jit(solution)/shard_map/dot_general | solution.py:25
  (1 shorter events, 0.0 us)
Async XLA Ops:
  6.5 123.5 %all-gather.3.cloned.1.call-start = ((), (), s32[]{:S(2)}) async-start(), calls=%async_computation.1 | async-start | bytes 17825792 | tf_op jit(solution)/shard_map/all_gather | solution.py:50
  10.3 216.9 %reduce-scatter.2.cloned.1.call-start = ((), (), s32[]{:S(2)}) async-start(), calls=%async_computation.2 | async-start | bytes 9437184 | tf_op jit(solution)/shard_map/reduce_scatter | solution.py:17
  138.8 180.7 %all-gather.5.cloned.1.call-start = ((), (), s32[]{:S(2)}) async-start(), calls=%async_computation.3 | async-start | bytes 9437184 | tf_op jit(solution)/shard_map/all_gather | solution.py:18
Sparse Core Ops, SparseCore 0:
  10.5 119.5 all-gather.2
  138.9 88.2 reduce-scatter.1
  228.9 90.5 all-gather.4
where the time goes:
time: 389 us; the launch traced here: 385 us
  waiting for transfers between devices  300 us (77%)
  matrix products  59.2 us (15%)
  between operations  13.1 us (3%)
  other arithmetic  12.4 us (3%)
    all_gather x1, waiting for transfers between devices, local(): lax.all_gather(scaled, 'col', axis=2, tiled=True)  120 us
    all_gather x1, waiting for transfers between devices, broadcast_by_parts(): lax.all_gather(own, axis, axis=0, tiled=True)[:len(lines)]  92.3 us
    reduce_scatter x1, waiting for transfers between devices, broadcast_by_parts(): own = lax.psum_scatter(padded, axis, scatter_dimension=0, tiled=True)  88.4 us
    dot_general x1, matrix products, tile_product(): lax.dot_general(flat_left, flat_right, (((0,), (0,)), ((), ())), precisio...  59.2 us
    select_n x1, other arithmetic, broadcast_by_parts(): jnp.where(lax.axis_index(axis) == root, value, jnp.zeros_like(value))  8.68 us
  transfers between devices with their start and end apart: 3, of which 3 were waited for; matrix products, arithmetic and copies ran while one was open for 0% of the time, Pallas kernels for 0%

commit v1 on v0

v1 whole, which is shorter than its diff:
```python
import functools

import jax
import jax.numpy as jnp
from jax import lax
from jax.experimental import pallas as pl
from jax.experimental.pallas import tpu as pltpu
from jax.sharding import PartitionSpec as P

MESH = pl.DeviceIdType.MESH
SAMPLES, FACTORS, BLOCK = 64, 32, 128
DEPTH = SAMPLES * FACTORS
PIECES = 8
ROWS = BLOCK // PIECES
DEEP = DEPTH // PIECES
PAIR = 2 * BLOCK


def place(a, b, y, z, c):
    return (b * 4 + z, a * 8 + y * 2 + c)


def kernel(
    x_ref,
    out_ref,
    rbuf,
    cbuf,
    csend,
    rhi,
    rlo,
    chi,
    clo,
    outbuf,
    send,
    t_recv,
    x_recv,
    b_recv,
    y1_recv,
    y2_recv,
    z1_recv,
    z2_recv,
    d_recv,
    out_sem,
):
    row, col = lax.axis_index("row"), lax.axis_index("col")
    b, z = row // 4, row % 4
    a, y, c = col // 8, (col // 2) % 4, col % 2
    up, down = 1, 3

    twin = place(a, b, y, z, 1 - c)
    across = place(1 - a, b, y, z, c)
    beside = place(a, 1 - b, y, z, c)
    y_dev = {d: place(a, b, (y + d) % 4, z, c) for d in (up, down)}
    z_dev = {d: place(a, b, y, (z + d) % 4, c) for d in (up, down)}
    t_to = place(b, 1 - c, z, (2 * z + 4 - y) % 4, a)
    t_from = place(c, a, (2 * y + 4 - z) % 4, y, 1 - b)

    def r_pair(flip, dy):
        return (a + flip) % 2 * 4 + (y + dy) % 4

    def c_pair(dz):
        return (2 * y + 8 - z - dz) % 4

    barrier = pltpu.get_barrier_semaphore()
    for device in (twin, across, beside, y_dev[up], y_dev[down], z_dev[up], z_dev[down], t_from):
        pl.semaphore_signal(barrier, inc=1, device_id=device, device_id_type=MESH)

    own = r_pair(0, 0) * 2 + c

    def normalise(i, _):
        x = x_ref[pl.ds(i * 8, 8)]
        variance = jnp.sum(x * x, axis=1, keepdims=True)
        scaled = (x * (1.0 / jnp.sqrt(variance))).reshape(8 * FACTORS, BLOCK)
        at = pl.ds(pl.multiple_of(i * 8 * FACTORS, 8 * FACTORS), 8 * FACTORS)
        csend[at, :] = scaled
        rbuf[own, :, at] = scaled.T
        return 0

    lax.fori_loop(0, SAMPLES // 8, normalise, 0)
    pl.semaphore_wait(barrier, 8)

    def go(src, dst, sem, recv, device):
        pltpu.make_async_remote_copy(
            src_ref=src, dst_ref=dst, send_sem=send.at[sem], recv_sem=recv, device_id=device, device_id_type=MESH
        ).start()

    def r_piece(block, i):
        return rbuf.at[block, pl.ds(i * ROWS, ROWS), :]

    def c_piece(block, i):
        return cbuf.at[block, pl.ds(i * DEEP, DEEP), :]

    def arrived(ref, sem):
        pltpu.make_async_copy(ref, ref, sem).wait()

    def r_go(block, i, sem, recv, device):
        go(r_piece(block, i), r_piece(block, i), sem, recv, device)

    def c_go(block, i, sem, recv, device):
        go(c_piece(block, i), c_piece(block, i), sem, recv, device)

    S_T, S_X, S_B, S_YU, S_YD, S_ZU, S_ZD, S_D = range(8)

    def hand_over(flip, dy):
        pair = r_pair(flip, dy)
        go(rbuf.at[pair * 2 + c], rbuf.at[pair * 2 + c], S_D, d_recv.at[pair], twin)

    def y_first(k, i):
        block = r_pair(k, 0) * 2 + c
        r_go(block, i, S_YU, y1_recv.at[0, k, i], y_dev[up])
        r_go(block, i, S_YD, y1_recv.at[1, k, i], y_dev[down])

    def z_first(k, block, i):
        c_go(block, i, S_ZU, z1_recv.at[0, k, i], z_dev[up])
        c_go(block, i, S_ZD, z1_recv.at[1, k, i], z_dev[down])

    def each(n, body):
        def step(i, _):
            body(i)
            return 0

        lax.fori_loop(0, n, step, 0)

    t_slot = y * 2 + c
    own_t = c_pair(0) * 2 + 1 - b
    own_b = c_pair(0) * 2 + b

    def start(i):
        go(csend.at[pl.ds(i * DEEP, DEEP), :], c_piece(t_slot, i), S_T, t_recv.at[i], t_to)
        r_go(own, i, S_X, x_recv.at[i], across)
        y_first(0, i)

    each(PIECES, start)
    hand_over(0, 0)

    def split_rows(pair, half):
        def body(i):
            at = pl.ds(pl.multiple_of(i * 16, 16), 16)
            v = rbuf[pair * 2 + half, at, :]
            hi = v.astype(jnp.bfloat16)
            to = pl.ds(pl.multiple_of(half * BLOCK + i * 16, 16), 16)
            rhi[pair, to, :] = hi
            rlo[pair, to, :] = (v - hi.astype(jnp.float32)).astype(jnp.bfloat16)

        each(BLOCK // 16, body)

    def ready_rows(flip, dy):
        pair = r_pair(flip, dy)
        arrived(rbuf.at[pair * 2 + 1 - c], d_recv.at[pair])
        split_rows(pair, 0)
        split_rows(pair, 1)

    def ready_columns(dz):
        pair = c_pair(dz)

        def body(i):
            at = pl.ds(pl.multiple_of(i * DEEP, DEEP), DEEP)
            for half in range(2):
                v = cbuf[pair * 2 + half, at, :]
                hi = v.astype(jnp.bfloat16)
                to = slice(half * BLOCK, (half + 1) * BLOCK)
                chi[pair, at, to] = hi
                clo[pair, at, to] = (v - hi.astype(jnp.float32)).astype(jnp.bfloat16)

        each(PIECES, body)

    def dot(left, right):
        return jnp.dot(left, right, preferred_element_type=jnp.float32)

    def tile(p, q):
        total = dot(rhi[p], chi[q]) + dot(rhi[p], clo[q]) + dot(rlo[p], chi[q])
        rows = pl.ds(pl.multiple_of(p * PAIR, PAIR), PAIR)
        columns = pl.ds(pl.multiple_of(q * PAIR, PAIR), PAIR)
        outbuf[rows, columns] = total * (1.0 / SAMPLES)
        pltpu.make_async_copy(outbuf.at[rows, columns], out_ref.at[rows, columns], out_sem).start()

    def turn(m):
        return m + m // 2 - 2 * (m // 3)

    ready_rows(0, 0)

    def relay(i):
        arrived(c_piece(own_t, i), t_recv.at[i])
        z_first(0, own_t, i)
        c_go(own_t, i, S_B, b_recv.at[i], beside)
        arrived(r_piece(r_pair(1, 0) * 2 + c, i), x_recv.at[i])
        y_first(1, i)

        @pl.when(i > 0)
        def _():
            arrived(c_piece(own_b, i - 1), b_recv.at[i - 1])
            z_first(1, own_b, i - 1)

    each(PIECES, relay)
    arrived(c_piece(own_b, PIECES - 1), b_recv.at[PIECES - 1])
    z_first(1, own_b, PIECES - 1)
    hand_over(1, 0)

    def y_second(k, half):
        even, odd = 2 * half, 2 * half + 1
        below, above = r_pair(k, down) * 2 + c, r_pair(k, up) * 2 + c
        for i in (even, odd):
            arrived(r_piece(below, i), y1_recv.at[0, k, i])
            arrived(r_piece(above, i), y1_recv.at[1, k, i])
        r_go(below, even, S_YU, y2_recv.at[0, k, half], y_dev[up])
        r_go(above, odd, S_YD, y2_recv.at[1, k, half], y_dev[down])

    def z_second(half):
        even, odd = 2 * half, 2 * half + 1
        for k in range(2):
            s = (1 - b + k) % 2
            below, above = c_pair(down) * 2 + s, c_pair(up) * 2 + s
            for i in (even, odd):
                arrived(c_piece(below, i), z1_recv.at[0, k, i])
                arrived(c_piece(above, i), z1_recv.at[1, k, i])
            c_go(below, even, S_ZU, z2_recv.at[0, k, half], z_dev[up])
            c_go(above, odd, S_ZD, z2_recv.at[1, k, half], z_dev[down])

    each(PIECES // 2, lambda half: y_second(0, half))
    hand_over(0, up)
    hand_over(0, down)
    ready_rows(1, 0)
    ready_columns(0)
    each(2, lambda k: tile(r_pair(k, 0), c_pair(0)))
    ready_rows(0, up)
    ready_rows(0, down)
    each(2, lambda k: tile(r_pair(0, 1 + 2 * k), c_pair(0)))

    def second(half):
        z_second(half)
        y_second(1, half)

    each(PIECES // 2, second)
    hand_over(1, up)
    hand_over(1, down)
    ready_columns(up)
    ready_columns(down)
    ready_rows(1, up)
    ready_rows(1, down)
    each(2, lambda k: tile(r_pair(1, 1 + 2 * k), c_pair(0)))
    each(12, lambda k: tile(r_pair(k % 2, turn(k // 2 % 3)), c_pair(1 + 2 * (k // 6))))

    def y_last(k):
        far = r_pair(k, 2) * 2 + c
        for half in range(PIECES // 2):
            arrived(r_piece(far, 2 * half), y2_recv.at[0, k, half])
            arrived(r_piece(far, 2 * half + 1), y2_recv.at[1, k, half])
        hand_over(k, 2)

    for k in range(2):
        y_last(k)
        ready_rows(k, 2)
        each(3, lambda m: tile(r_pair(k, 2), c_pair(turn(m))))

    for k in range(2):
        far = c_pair(2) * 2 + (1 - b + k) % 2
        for half in range(PIECES // 2):
            arrived(c_piece(far, 2 * half), z2_recv.at[0, k, half])
            arrived(c_piece(far, 2 * half + 1), z2_recv.at[1, k, half])
    ready_columns(2)
    each(8, lambda k: tile(k, c_pair(2)))

    for sem, blocks in ((S_T, 1), (S_X, 1), (S_B, 1), (S_YU, 3), (S_YD, 3), (S_ZU, 3), (S_ZD, 3), (S_D, 8)):
        arrived(rbuf.at[pl.ds(0, blocks)], send.at[sem])
    pltpu.make_async_copy(outbuf, out_ref, out_sem).wait()


def local(loadings):
    dma = pltpu.SemaphoreType.DMA
    return pl.pallas_call(
        kernel,
        out_shape=jax.ShapeDtypeStruct((16 * BLOCK, 8 * BLOCK), jnp.float32),
        in_specs=[pl.BlockSpec(memory_space=pltpu.VMEM)],
        out_specs=pl.BlockSpec(memory_space=pl.ANY),
        scratch_shapes=[
            pltpu.VMEM((16, BLOCK, DEPTH), jnp.float32),
            pltpu.VMEM((8, DEPTH, BLOCK), jnp.float32),
            pltpu.VMEM((DEPTH, BLOCK), jnp.float32),
            pltpu.VMEM((8, PAIR, DEPTH), jnp.bfloat16),
            pltpu.VMEM((8, PAIR, DEPTH), jnp.bfloat16),
            pltpu.VMEM((4, DEPTH, PAIR), jnp.bfloat16),
            pltpu.VMEM((4, DEPTH, PAIR), jnp.bfloat16),
            pltpu.VMEM((16 * BLOCK, 8 * BLOCK), jnp.float32),
            dma((8,)),
            dma((PIECES,)),
            dma((PIECES,)),
            dma((PIECES,)),
            dma((2, 2, PIECES)),
            dma((2, 2, PIECES // 2)),
            dma((2, 2, PIECES)),
            dma((2, 2, PIECES // 2)),
            dma((8,)),
            dma,
        ],
        compiler_params=pltpu.CompilerParams(
            collective_id=0, has_side_effects=True, vmem_limit_bytes=61 * 1024 * 1024
        ),
    )(loadings)


def solution(mesh):
    placed = (P(None, None, ("row", "col")),)
    return jax.shard_map(local, mesh=mesh, in_specs=placed, out_specs=P("row", "col"), check_vma=False)
```

time: 389 us -> 159 us (0.41)
  the two profiles are of different devices: /device:TPU:35 before, /device:TPU:7 now
where the time goes in v1:
time: 159 us
  Pallas kernels  150 us (94%)
  local copies, waits for them, and re-layouts  8.44 us (5%)
    pallas_call x1, Pallas kernels, local(): pl.pallas_call(kernel, out_shape=jax.ShapeDtypeStruct((16 * BLOCK, 8 * BL...  150 us
    unnamed x1, local copies, waits for them, and re-layouts  8.44 us

profile of v1, /device:TPU:7, one launch (start us, length us, event | category | flops | bytes accessed | tf_op | source)
XLA Modules:
  0.0 158.8 jit_solution(10115655663990300083)
XLA Ops:
  0.0 150.3 %shard_map.17 = f32[2048,1024]{1,0:T(8,128)} custom-call(f32[64,32,128]{2,1,0:T(8,128)} %x_ref.1), custom_call_target="tpu_custom_call" | custom-call | tf_op jit(solution)/shard_map/pallas_call | solution.py:270
  150.3 8.4 %copy.3 = f32[2048,1024]{1,0:T(8,128)} copy(f32[2048,1024]{1,0:T(8,128)} %shard_map.17) | data formatting | bytes 16777216

commit v2 on v1

v2 whole, which is shorter than its diff:
```python
import functools

import jax
import jax.numpy as jnp
from jax import lax
from jax.experimental import pallas as pl
from jax.experimental.pallas import tpu as pltpu
from jax.sharding import PartitionSpec as P

MESH = pl.DeviceIdType.MESH
SAMPLES, FACTORS, BLOCK = 64, 32, 128
DEPTH = SAMPLES * FACTORS
PIECES = 8
ROWS = BLOCK // PIECES
DEEP = DEPTH // PIECES
PAIR = 2 * BLOCK


def place(a, b, y, z, c):
    return (b * 4 + z, a * 8 + y * 2 + c)


def kernel(
    x_ref,
    out_ref,
    rbuf,
    cbuf,
    csend,
    tbuf,
    rhi,
    rlo,
    chi,
    clo,
    outbuf,
    send,
    t_recv,
    tr_recv,
    x_recv,
    b_recv,
    y1_recv,
    y2_recv,
    z1_recv,
    z2_recv,
    d_recv,
    out_sem,
):
    row, col = lax.axis_index("row"), lax.axis_index("col")
    b, z = row // 4, row % 4
    a, y, c = col // 8, (col // 2) % 4, col % 2
    up, down = 1, 3

    twin = place(a, b, y, z, 1 - c)
    across = place(1 - a, b, y, z, c)
    beside = place(a, 1 - b, y, z, c)
    y_dev = {d: place(a, b, (y + d) % 4, z, c) for d in (up, down)}
    z_dev = {d: place(a, b, y, (z + d) % 4, c) for d in (up, down)}
    t_to = place(b, 1 - c, z, (2 * z + 4 - y) % 4, a)
    t_from = place(c, a, (2 * y + 4 - z) % 4, y, 1 - b)
    off = (y + 4 - z) % 4
    turns = (1, 3)

    def corner_from(e):
        return place(c, a, (y + 6 - e) % 4, (z + 4 - e) % 4, 1 - b)

    def corner_to(e):
        return place(a, b, (y + 4 - e) % 4, (z + 6 - e) % 4, c)

    def side_from(d):
        return place(c, a, y, (y + 4 - d) % 4, 1 - b)

    def side_to(d):
        return place(a, b, (y + 4 - d) % 4, z, c)

    def r_pair(flip, dy):
        return (a + flip) % 2 * 4 + (y + dy) % 4

    def c_pair(dz):
        return (2 * y + 8 - z - dz) % 4

    barrier = pltpu.get_barrier_semaphore()

    def here(*devices):
        for device in devices:
            pl.semaphore_signal(barrier, inc=1, device_id=device, device_id_type=MESH)

    here(twin, across, beside, y_dev[up], y_dev[down], z_dev[up], z_dev[down], t_from)

    @pl.when(off % 2 == 1)
    def _():
        here(place(a, b, (y + off) % 4, z, c))

    @pl.when(off == 2)
    def _():
        here(*(side_from(d) for d in turns))
        here(*(place(a, b, (y + e) % 4, (y + e) % 4, c) for e in turns))

    @pl.when(off == 0)
    def _():
        here(*(corner_from(e) for e in turns))

    own = r_pair(0, 0) * 2 + c

    def normalise(i, _):
        x = x_ref[pl.ds(i * 8, 8)]
        variance = jnp.sum(x * x, axis=1, keepdims=True)
        scaled = (x * (1.0 / jnp.sqrt(variance))).reshape(8 * FACTORS, BLOCK)
        at = pl.ds(pl.multiple_of(i * 8 * FACTORS, 8 * FACTORS), 8 * FACTORS)
        csend[at, :] = scaled
        rbuf[own, :, at] = scaled.T
        return 0

    lax.fori_loop(0, SAMPLES // 8, normalise, 0)
    odd = off % 2
    pl.semaphore_wait(barrier, 8 + odd + (1 - odd) * (2 + 2 * (off // 2)))

    def go(src, dst, sem, recv, device):
        pltpu.make_async_remote_copy(
            src_ref=src, dst_ref=dst, send_sem=send.at[sem], recv_sem=recv, device_id=device, device_id_type=MESH
        ).start()

    def r_piece(block, i):
        return rbuf.at[block, pl.ds(i * ROWS, ROWS), :]

    def c_piece(block, i):
        return cbuf.at[block, pl.ds(i * DEEP, DEEP), :]

    def arrived(ref, sem):
        pltpu.make_async_copy(ref, ref, sem).wait()

    def r_go(block, i, sem, recv, device):
        go(r_piece(block, i), r_piece(block, i), sem, recv, device)

    def c_go(block, i, sem, recv, device):
        go(c_piece(block, i), c_piece(block, i), sem, recv, device)

    S_T, S_X, S_B, S_YU, S_YD, S_ZU, S_ZD, S_D, S_TR = range(9)

    def hand_over(flip, dy):
        pair = r_pair(flip, dy)
        go(rbuf.at[pair * 2 + c], rbuf.at[pair * 2 + c], S_D, d_recv.at[pair], twin)

    def y_first(k, i):
        block = r_pair(k, 0) * 2 + c
        r_go(block, i, S_YU, y1_recv.at[0, k, i], y_dev[up])
        r_go(block, i, S_YD, y1_recv.at[1, k, i], y_dev[down])

    def z_first(k, block, i):
        c_go(block, i, S_ZU, z1_recv.at[0, k, i], z_dev[up])
        c_go(block, i, S_ZD, z1_recv.at[1, k, i], z_dev[down])

    def each(n, body):
        def step(i, _):
            body(i)
            return 0

        lax.fori_loop(0, n, step, 0)

    t_slot = y * 2 + c
    own_t = c_pair(0) * 2 + 1 - b
    own_b = c_pair(0) * 2 + b

    def transposed(i):
        src = csend.at[pl.ds(i * DEEP, DEEP), :]
        aside = (off % 2) * (i % 4 // 3) + (off // 2) * (1 - off % 2)
        f, slot = i % 2, i // 2

        @pl.when(aside == 0)
        def _():
            go(src, c_piece(t_slot, i), S_T, t_recv.at[i], t_to)

        @pl.when(aside * (off % 2) == 1)
        def _():
            g = off // 2
            go(src, tbuf.at[g, i // 4], S_T, tr_recv.at[g, i // 4], place(b, 1 - c, y, (z + 4 - off) % 4, a))

        @pl.when(aside * (1 - off % 2) == 1)
        def _():
            w = (z + 1 + 2 * f) % 4
            go(src, tbuf.at[f, slot], S_T, tr_recv.at[f, slot], place(b, 1 - c, w, w, a))

    def start(i):
        y_first(0, i)

    def pass_corner(i):
        f, slot = i % 2, i // 2

        @pl.when(off == 0)
        def _():
            e = 1 + 2 * f
            arrived(tbuf.at[f, slot], tr_recv.at[f, slot])
            at = (y + 6 - e) % 4 * 2 + 1 - b
            go(tbuf.at[f, slot], c_piece(at, i), S_TR, t_recv.at[i], corner_to(e))

    def pass_side(i):
        f, slot = i % 2, i // 2

        @pl.when((off // 2) * (1 - off % 2) * (1 - i // 4) == 1)
        def _():
            arrived(tbuf.at[f, slot], tr_recv.at[f, slot])
            p = 4 * slot + 3
            go(tbuf.at[f, slot], c_piece(y * 2 + 1 - b, p), S_TR, t_recv.at[p], side_to(1 + 2 * f))

    each(PIECES, transposed)
    each(PIECES, start)
    hand_over(0, 0)

    def split_rows(pair, half):
        def body(i):
            at = pl.ds(pl.multiple_of(i * 16, 16), 16)
            v = rbuf[pair * 2 + half, at, :]
            hi = v.astype(jnp.bfloat16)
            to = pl.ds(pl.multiple_of(pair * PAIR + half * BLOCK + i * 16, 16), 16)
            rhi[to, :] = hi
            rlo[to, :] = (v - hi.astype(jnp.float32)).astype(jnp.bfloat16)

        each(BLOCK // 16, body)

    def ready_rows(flip, dy):
        pair = r_pair(flip, dy)
        arrived(rbuf.at[pair * 2 + 1 - c], d_recv.at[pair])
        split_rows(pair, 0)
        split_rows(pair, 1)

    def blocks_of(slot):
        beyond = (slot + 1) // 2
        which = (slot + b) % 2
        left = (1 - beyond) * (c_pair(0) * 2) + beyond * (c_pair(up) * 2 + which)
        right = (1 - beyond) * (c_pair(0) * 2 + 1) + beyond * (c_pair(down) * 2 + which)
        return left, right

    def ready_columns(slot):
        for side, block in enumerate(blocks_of(slot)):

            def body(i):
                at = pl.ds(pl.multiple_of(i * DEEP, DEEP), DEEP)
                v = cbuf[block, at, :]
                hi = v.astype(jnp.bfloat16)
                to = slice(side * BLOCK, (side + 1) * BLOCK)
                chi[slot, at, to] = hi
                clo[slot, at, to] = (v - hi.astype(jnp.float32)).astype(jnp.bfloat16)

            each(PIECES, body)

    def dot(left, right):
        return jnp.dot(left, right, preferred_element_type=jnp.float32)

    def tile(p, slot):
        rows = pl.ds(pl.multiple_of(p * PAIR, PAIR), PAIR)
        right = chi[slot]
        total = dot(rhi[rows, :], right) + dot(rhi[rows, :], clo[slot]) + dot(rlo[rows, :], right)
        total = total * (1.0 / SAMPLES)
        for side, block in enumerate(blocks_of(slot)):
            columns = pl.ds(pl.multiple_of(block * BLOCK, BLOCK), BLOCK)
            outbuf[rows, columns] = total[:, side * BLOCK : (side + 1) * BLOCK]
            pltpu.make_async_copy(outbuf.at[rows, columns], out_ref.at[rows, columns], out_sem).start()

    def turn(m):
        return m + m // 2 - 2 * (m // 3)

    ready_rows(0, 0)

    def y_second(k, half):
        even, odd = 2 * half, 2 * half + 1
        below, above = r_pair(k, down) * 2 + c, r_pair(k, up) * 2 + c
        for i in (even, odd):
            arrived(r_piece(below, i), y1_recv.at[0, k, i])
            arrived(r_piece(above, i), y1_recv.at[1, k, i])
        r_go(below, even, S_YU, y2_recv.at[0, k, half], y_dev[up])
        r_go(above, odd, S_YD, y2_recv.at[1, k, half], y_dev[down])

    def z_second(k, half):
        even, odd = 2 * half, 2 * half + 1
        s = (1 - b + k) % 2
        below, above = c_pair(down) * 2 + s, c_pair(up) * 2 + s
        for i in (even, odd):
            arrived(c_piece(below, i), z1_recv.at[0, k, i])
            arrived(c_piece(above, i), z1_recv.at[1, k, i])
        c_go(below, even, S_ZU, z2_recv.at[0, k, half], z_dev[up])
        c_go(above, odd, S_ZD, z2_recv.at[1, k, half], z_dev[down])

    def early(i):
        @pl.when((off // 2) * (1 - off % 2) * (i % 2) == 1)
        def _():
            z_second(0, i // 2)

        pass_side(i)
        arrived(c_piece(own_t, i), t_recv.at[i])
        z_first(0, own_t, i)
        c_go(own_t, i, S_B, b_recv.at[i], beside)
        r_go(own, i, S_X, x_recv.at[i], across)
        pass_corner(i)

        @pl.when(i >= PIECES // 2)
        def _():
            y_second(0, i - PIECES // 2)

            @pl.when(off == 0)
            def _():
                z_second(0, i - PIECES // 2)

    each(PIECES, early)

    def middle(i):
        arrived(r_piece(r_pair(1, 0) * 2 + c, i), x_recv.at[i])
        y_first(1, i)

        @pl.when((i % 2) * (off % 2) == 1)
        def _():
            z_second(0, i // 2)

        arrived(c_piece(own_b, i), b_recv.at[i])
        z_first(1, own_b, i)

    each(PIECES, middle)
    hand_over(0, up)
    hand_over(0, down)
    hand_over(1, 0)
    ready_columns(0)
    ready_columns(1)

    def y_last(k):
        far = r_pair(k, 2) * 2 + c
        for half in range(PIECES // 2):
            arrived(r_piece(far, 2 * half), y2_recv.at[0, k, half])
            arrived(r_piece(far, 2 * half + 1), y2_recv.at[1, k, half])
        hand_over(k, 2)

    for half in range(PIECES // 2):
        y_second(1, half)
        flip, dy = ((0, 0), (0, up), (0, down), (1, 0))[half]
        if half:
            ready_rows(flip, dy)
        each(2, lambda slot: tile(r_pair(flip, dy), slot))
    hand_over(1, up)
    hand_over(1, down)
    for half in range(PIECES // 2):
        z_second(1, half)
        if half == 0:
            y_last(0)
        else:
            flip, dy = ((1, up), (1, down), (0, 2))[half - 1]
            ready_rows(flip, dy)
            each(2, lambda slot: tile(r_pair(flip, dy), slot))
    ready_columns(2)
    y_last(1)
    each(7, lambda t: tile(r_pair(t % 2, turn(t // 2)), 2))
    ready_rows(1, 2)
    each(3, lambda slot: tile(r_pair(1, 2), slot))

    q = c_pair(2)
    columns = pl.ds(pl.multiple_of(q * PAIR, PAIR), PAIR)
    for half in range(PIECES // 2):
        for k in range(2):
            arrived(c_piece(q * 2 + k, 2 * half), z2_recv.at[0, (k + b + 1) % 2, half])
            arrived(c_piece(q * 2 + k, 2 * half + 1), z2_recv.at[1, (k + b + 1) % 2, half])
        deep = slice(2 * half * DEEP, 2 * (half + 1) * DEEP)
        for k in range(2):
            to = slice(k * BLOCK, (k + 1) * BLOCK)
            v = cbuf[q * 2 + k, deep, :]
            hi = v.astype(jnp.bfloat16)
            chi[3, deep, to] = hi
            clo[3, deep, to] = (v - hi.astype(jnp.float32)).astype(jnp.bfloat16)

        def part(m):
            rows = pl.ds(pl.multiple_of(m * 2 * PAIR, 2 * PAIR), 2 * PAIR)
            left, right = rhi[rows, deep], chi[3, deep, :]
            total = dot(left, right) + dot(left, clo[3, deep, :]) + dot(rlo[rows, deep], right)
            total = total * (1.0 / SAMPLES)
            outbuf[rows, columns] = total if half == 0 else outbuf[rows, columns] + total
            if half == PIECES // 2 - 1:
                pltpu.make_async_copy(outbuf.at[rows, columns], out_ref.at[rows, columns], out_sem).start()

        each(4, part)

    for sem, blocks in ((S_T, 1), (S_X, 1), (S_B, 1), (S_YU, 3), (S_YD, 3), (S_ZU, 3), (S_ZD, 3), (S_D, 8)):
        arrived(rbuf.at[pl.ds(0, blocks)], send.at[sem])

    @pl.when(off == 0)
    def _():
        arrived(rbuf.at[0], send.at[S_TR])

    @pl.when(off == 2)
    def _():
        arrived(rbuf.at[0, pl.ds(0, BLOCK // 2), :], send.at[S_TR])

    pltpu.make_async_copy(outbuf, out_ref, out_sem).wait()


def local(loadings):
    dma = pltpu.SemaphoreType.DMA
    return pl.pallas_call(
        kernel,
        out_shape=jax.ShapeDtypeStruct((16 * BLOCK, 8 * BLOCK), jnp.float32),
        in_specs=[pl.BlockSpec(memory_space=pltpu.VMEM)],
        out_specs=pl.BlockSpec(memory_space=pl.ANY),
        scratch_shapes=[
            pltpu.VMEM((16, BLOCK, DEPTH), jnp.float32),
            pltpu.VMEM((8, DEPTH, BLOCK), jnp.float32),
            pltpu.VMEM((DEPTH, BLOCK), jnp.float32),
            pltpu.VMEM((2, PIECES // 2, DEEP, BLOCK), jnp.float32),
            pltpu.VMEM((8 * PAIR, DEPTH), jnp.bfloat16),
            pltpu.VMEM((8 * PAIR, DEPTH), jnp.bfloat16),
            pltpu.VMEM((4, DEPTH, PAIR), jnp.bfloat16),
            pltpu.VMEM((4, DEPTH, PAIR), jnp.bfloat16),
            pltpu.VMEM((16 * BLOCK, 8 * BLOCK), jnp.float32),
            dma((9,)),
            dma((PIECES,)),
            dma((2, PIECES // 2)),
            dma((PIECES,)),
            dma((PIECES,)),
            dma((2, 2, PIECES)),
            dma((2, 2, PIECES // 2)),
            dma((2, 2, PIECES)),
            dma((2, 2, PIECES // 2)),
            dma((8,)),
            dma,
        ],
        compiler_params=pltpu.CompilerParams(
            collective_id=0, has_side_effects=True, vmem_limit_bytes=61 * 1024 * 1024
        ),
    )(loadings)


def solution(mesh):
    placed = (P(None, None, ("row", "col")),)
    return jax.shard_map(local, mesh=mesh, in_specs=placed, out_specs=P("row", "col"), check_vma=False)
```

time: 159 us -> 138 us (0.87)
  the two profiles are of different devices: /device:TPU:7 before, /device:TPU:35 now
where the time goes in v2:
time: 138 us; the launch traced here: 137 us
  Pallas kernels  129 us (93%)
  local copies, waits for them, and re-layouts  8.44 us (6%)
    pallas_call x1, Pallas kernels, local(): pl.pallas_call(kernel, out_shape=jax.ShapeDtypeStruct((16 * BLOCK, 8 * BL...  129 us
    unnamed x1, local copies, waits for them, and re-layouts  8.44 us

profile of v2, /device:TPU:35, one launch (start us, length us, event | category | flops | bytes accessed | tf_op | source)
XLA Modules:
  0.0 137.4 jit_solution(9321906253667744372)
XLA Ops:
  0.0 129.0 %shard_map.17 = f32[2048,1024]{1,0:T(8,128)} custom-call(f32[64,32,128]{2,1,0:T(8,128)} %x_ref.1), custom_call_target="tpu_custom_call" | custom-call | tf_op jit(solution)/shard_map/pallas_call | solution.py:391
  129.0 8.4 %copy.3 = f32[2048,1024]{1,0:T(8,128)} copy(f32[2048,1024]{1,0:T(8,128)} %shard_map.17) | data formatting | bytes 16777216

commit v3 on v2

--- a/solution.py
+++ b/solution.py
@@ -22,7 +22,7 @@
 
 def kernel(
     x_ref,
-    out_ref,
+    outbuf,
     rbuf,
     cbuf,
     csend,
@@ -31,7 +31,6 @@
     rlo,
     chi,
     clo,
-    outbuf,
     send,
     t_recv,
     tr_recv,
@@ -42,7 +41,6 @@
     z1_recv,
     z2_recv,
     d_recv,
-    out_sem,
 ):
     row, col = lax.axis_index("row"), lax.axis_index("col")
     b, z = row // 4, row % 4
@@ -179,7 +177,9 @@
             go(src, tbuf.at[f, slot], S_T, tr_recv.at[f, slot], place(b, 1 - c, w, w, a))
 
     def start(i):
-        y_first(0, i)
+        @pl.when(i < 3)
+        def _():
+            y_first(0, i)
 
     def pass_corner(i):
         f, slot = i % 2, i // 2
@@ -252,7 +252,6 @@
         for side, block in enumerate(blocks_of(slot)):
             columns = pl.ds(pl.multiple_of(block * BLOCK, BLOCK), BLOCK)
             outbuf[rows, columns] = total[:, side * BLOCK : (side + 1) * BLOCK]
-            pltpu.make_async_copy(outbuf.at[rows, columns], out_ref.at[rows, columns], out_sem).start()
 
     def turn(m):
         return m + m // 2 - 2 * (m // 3)
@@ -289,6 +288,10 @@
         c_go(own_t, i, S_B, b_recv.at[i], beside)
         r_go(own, i, S_X, x_recv.at[i], across)
         pass_corner(i)
+
+        @pl.when(i < PIECES - 3)
+        def _():
+            y_first(0, i + 3)
 
         @pl.when(i >= PIECES // 2)
         def _():
@@ -367,8 +370,6 @@
             total = dot(left, right) + dot(left, clo[3, deep, :]) + dot(rlo[rows, deep], right)
             total = total * (1.0 / SAMPLES)
             outbuf[rows, columns] = total if half == 0 else outbuf[rows, columns] + total
-            if half == PIECES // 2 - 1:
-                pltpu.make_async_copy(outbuf.at[rows, columns], out_ref.at[rows, columns], out_sem).start()
 
         each(4, part)
 
@@ -383,16 +384,21 @@
     def _():
         arrived(rbuf.at[0, pl.ds(0, BLOCK // 2), :], send.at[S_TR])
 
-    pltpu.make_async_copy(outbuf, out_ref, out_sem).wait()
+
+def write_out(held, out_ref, sem):
+    for i in range(8):
+        rows = pl.ds(i * PAIR, PAIR)
+        pltpu.make_async_copy(held.at[rows], out_ref.at[rows], sem).start()
+    pltpu.make_async_copy(held, out_ref, sem).wait()
 
 
 def local(loadings):
     dma = pltpu.SemaphoreType.DMA
-    return pl.pallas_call(
+    held = pl.pallas_call(
         kernel,
-        out_shape=jax.ShapeDtypeStruct((16 * BLOCK, 8 * BLOCK), jnp.float32),
+        out_shape=pltpu.VMEM((16 * BLOCK, 8 * BLOCK), jnp.float32),
         in_specs=[pl.BlockSpec(memory_space=pltpu.VMEM)],
-        out_specs=pl.BlockSpec(memory_space=pl.ANY),
+        out_specs=pl.BlockSpec(memory_space=pltpu.VMEM),
         scratch_shapes=[
             pltpu.VMEM((16, BLOCK, DEPTH), jnp.float32),
             pltpu.VMEM((8, DEPTH, BLOCK), jnp.float32),
@@ -402,7 +408,6 @@
             pltpu.VMEM((8 * PAIR, DEPTH), jnp.bfloat16),
             pltpu.VMEM((4, DEPTH, PAIR), jnp.bfloat16),
             pltpu.VMEM((4, DEPTH, PAIR), jnp.bfloat16),
-            pltpu.VMEM((16 * BLOCK, 8 * BLOCK), jnp.float32),
             dma((9,)),
             dma((PIECES,)),
             dma((2, PIECES // 2)),
@@ -413,12 +418,19 @@
             dma((2, 2, PIECES)),
             dma((2, 2, PIECES // 2)),
             dma((8,)),
-            dma,
         ],
         compiler_params=pltpu.CompilerParams(
-            collective_id=0, has_side_effects=True, vmem_limit_bytes=61 * 1024 * 1024
+            collective_id=0, has_side_effects=True, vmem_limit_bytes=54 * 1024 * 1024
         ),
     )(loadings)
+    return pl.pallas_call(
+        write_out,
+        out_shape=jax.ShapeDtypeStruct(held.shape, held.dtype),
+        in_specs=[pl.BlockSpec(memory_space=pltpu.VMEM)],
+        out_specs=pl.BlockSpec(memory_space=pl.ANY),
+        scratch_shapes=[dma],
+        compiler_params=pltpu.CompilerParams(vmem_limit_bytes=1024 * 1024),
+    )(held)
 
 
 def solution(mesh):

time: 138 us -> 125 us (0.906)
  local copies, waits for them, and re-layouts: 8.44 us -> 0 us
  Pallas kernels: 129 us -> 125 us
    unnamed x1 -> x0, local copies, waits for them, and re-layouts: 8.44 us -> none
    pallas_call x1 -> x2, Pallas kernels: 129 us -> 125 us  [the longest x1 121 us: local(): pl.pallas_call(kernel, out_shape=pltpu.VMEM((16 * BLOCK, 8 * BLOCK), jnp....]
where the time goes in v3:
time: 125 us
  Pallas kernels  125 us (100%)
    pallas_call x1, Pallas kernels, local(): pl.pallas_call(kernel, out_shape=pltpu.VMEM((16 * BLOCK, 8 * BLOCK), jnp....  121 us
    pallas_call x1, Pallas kernels, local(): pl.pallas_call(write_out, out_shape=jax.ShapeDtypeStruct(held.shape, held...  3.31 us

profile of v3, /device:TPU:35, one launch (start us, length us, event | category | flops | bytes accessed | tf_op | source)
XLA Modules:
  0.0 124.5 jit_solution(11470898606324349050)
XLA Ops:
  0.0 121.2 %shard_map.17.held = f32[2048,1024]{1,0:T(8,128)S(1)} custom-call(f32[64,32,128]{2,1,0:T(8,128)} %x_ref.1), custom_call_target="tpu_custom_call" | custom-call | tf_op jit(solution)/shard_map/pallas_call | solution.py:397
  121.2 3.3 %shard_map.18 = f32[2048,1024]{1,0:T(8,128)} custom-call(f32[2048,1024]{1,0:T(8,128)S(1)} %shard_map.17.held), custom_call_target="tpu_custom_call" | custom-call | tf_op jit(solution)/shard_map/pallas_call | solution.py:426

commit v4 on v3

--- a/solution.py
+++ b/solution.py
@@ -228,30 +228,32 @@
         right = (1 - beyond) * (c_pair(0) * 2 + 1) + beyond * (c_pair(down) * 2 + which)
         return left, right
 
+    def split_columns(species, slot, side, i):
+        at = pl.ds(pl.multiple_of(i * DEEP, DEEP), DEEP)
+        v = cbuf[species, at, :]
+        hi = v.astype(jnp.bfloat16)
+        to = slice(side * BLOCK, (side + 1) * BLOCK)
+        chi[slot, at, to] = hi
+        clo[slot, at, to] = (v - hi.astype(jnp.float32)).astype(jnp.bfloat16)
+
     def ready_columns(slot):
-        for side, block in enumerate(blocks_of(slot)):
-
-            def body(i):
-                at = pl.ds(pl.multiple_of(i * DEEP, DEEP), DEEP)
-                v = cbuf[block, at, :]
-                hi = v.astype(jnp.bfloat16)
-                to = slice(side * BLOCK, (side + 1) * BLOCK)
-                chi[slot, at, to] = hi
-                clo[slot, at, to] = (v - hi.astype(jnp.float32)).astype(jnp.bfloat16)
-
-            each(PIECES, body)
+        for side, species in enumerate(blocks_of(slot)):
+            each(PIECES, lambda i: split_columns(species, slot, side, i))
 
     def dot(left, right):
         return jnp.dot(left, right, preferred_element_type=jnp.float32)
 
-    def tile(p, slot):
-        rows = pl.ds(pl.multiple_of(p * PAIR, PAIR), PAIR)
+    def block(start, n, slot, columns_of):
+        rows = pl.ds(pl.multiple_of(start * PAIR, PAIR), n * PAIR)
         right = chi[slot]
         total = dot(rhi[rows, :], right) + dot(rhi[rows, :], clo[slot]) + dot(rlo[rows, :], right)
         total = total * (1.0 / SAMPLES)
-        for side, block in enumerate(blocks_of(slot)):
-            columns = pl.ds(pl.multiple_of(block * BLOCK, BLOCK), BLOCK)
+        for side, species in enumerate(columns_of):
+            columns = pl.ds(pl.multiple_of(species * BLOCK, BLOCK), BLOCK)
             outbuf[rows, columns] = total[:, side * BLOCK : (side + 1) * BLOCK]
+
+    def tile(p, slot):
+        block(p, 1, slot, blocks_of(slot))
 
     def turn(m):
         return m + m // 2 - 2 * (m // 3)
@@ -344,34 +346,23 @@
             flip, dy = ((1, up), (1, down), (0, 2))[half - 1]
             ready_rows(flip, dy)
             each(2, lambda slot: tile(r_pair(flip, dy), slot))
+    y_last(1)
     ready_columns(2)
-    y_last(1)
-    each(7, lambda t: tile(r_pair(t % 2, turn(t // 2)), 2))
+    last = r_pair(1, 2)
+    each(3, lambda m: block((last // 2 + 1 + m) % 4 * 2, 2, 2, blocks_of(2)))
     ready_rows(1, 2)
-    each(3, lambda slot: tile(r_pair(1, 2), slot))
-
-    q = c_pair(2)
-    columns = pl.ds(pl.multiple_of(q * PAIR, PAIR), PAIR)
-    for half in range(PIECES // 2):
-        for k in range(2):
-            arrived(c_piece(q * 2 + k, 2 * half), z2_recv.at[0, (k + b + 1) % 2, half])
-            arrived(c_piece(q * 2 + k, 2 * half + 1), z2_recv.at[1, (k + b + 1) % 2, half])
-        deep = slice(2 * half * DEEP, 2 * (half + 1) * DEEP)
-        for k in range(2):
-            to = slice(k * BLOCK, (k + 1) * BLOCK)
-            v = cbuf[q * 2 + k, deep, :]
-            hi = v.astype(jnp.bfloat16)
-            chi[3, deep, to] = hi
-            clo[3, deep, to] = (v - hi.astype(jnp.float32)).astype(jnp.bfloat16)
-
-        def part(m):
-            rows = pl.ds(pl.multiple_of(m * 2 * PAIR, 2 * PAIR), 2 * PAIR)
-            left, right = rhi[rows, deep], chi[3, deep, :]
-            total = dot(left, right) + dot(left, clo[3, deep, :]) + dot(rlo[rows, deep], right)
-            total = total * (1.0 / SAMPLES)
-            outbuf[rows, columns] = total if half == 0 else outbuf[rows, columns] + total
-
-        each(4, part)
+    block(last // 2 * 2, 2, 2, blocks_of(2))
+    each(2, lambda slot: tile(last, slot))
+
+    far = (c_pair(2) * 2, c_pair(2) * 2 + 1)
+    for k in range(2):
+        species = c_pair(2) * 2 + (1 - b + k) % 2
+        for half in range(PIECES // 2):
+            arrived(c_piece(species, 2 * half), z2_recv.at[0, k, half])
+            arrived(c_piece(species, 2 * half + 1), z2_recv.at[1, k, half])
+    for side in range(2):
+        each(PIECES, lambda i: split_columns(far[side], 0, side, i))
+    each(4, lambda m: block(m * 2, 2, 0, far))
 
     for sem, blocks in ((S_T, 1), (S_X, 1), (S_B, 1), (S_YU, 3), (S_YD, 3), (S_ZU, 3), (S_ZD, 3), (S_D, 8)):
         arrived(rbuf.at[pl.ds(0, blocks)], send.at[sem])
@@ -406,8 +397,8 @@
             pltpu.VMEM((2, PIECES // 2, DEEP, BLOCK), jnp.float32),
             pltpu.VMEM((8 * PAIR, DEPTH), jnp.bfloat16),
             pltpu.VMEM((8 * PAIR, DEPTH), jnp.bfloat16),
-            pltpu.VMEM((4, DEPTH, PAIR), jnp.bfloat16),
-            pltpu.VMEM((4, DEPTH, PAIR), jnp.bfloat16),
+            pltpu.VMEM((3, DEPTH, PAIR), jnp.bfloat16),
+            pltpu.VMEM((3, DEPTH, PAIR), jnp.bfloat16),
             dma((9,)),
             dma((PIECES,)),
             dma((2, PIECES // 2)),

time: 125 us -> 122 us (0.976)
  Pallas kernels: 125 us -> 122 us
    pallas_call x1, Pallas kernels: 121 us -> 119 us  [local(): pl.pallas_call(kernel, out_shape=pltpu.VMEM((16 * BLOCK, 8 * BLOCK), jnp....]
where the time goes in v4:
time: 122 us
  Pallas kernels  122 us (100%)
    pallas_call x1, Pallas kernels, local(): pl.pallas_call(kernel, out_shape=pltpu.VMEM((16 * BLOCK, 8 * BLOCK), jnp....  119 us
    pallas_call x1, Pallas kernels, local(): pl.pallas_call(write_out, out_shape=jax.ShapeDtypeStruct(held.shape, held...  3.31 us

profile of v4, /device:TPU:35, one launch (start us, length us, event | category | flops | bytes accessed | tf_op | source)
XLA Modules:
  0.0 122.0 jit_solution(5443044150205643008)
XLA Ops:
  0.0 118.7 %shard_map.17.held = f32[2048,1024]{1,0:T(8,128)S(1)} custom-call(f32[64,32,128]{2,1,0:T(8,128)} %x_ref.1), custom_call_target="tpu_custom_call" | custom-call | tf_op jit(solution)/shard_map/pallas_call | solution.py:388
  118.7 3.3 %shard_map.18 = f32[2048,1024]{1,0:T(8,128)} custom-call(f32[2048,1024]{1,0:T(8,128)S(1)} %shard_map.17.held), custom_call_target="tpu_custom_call" | custom-call | tf_op jit(solution)/shard_map/pallas_call | solution.py:417

commit v5 on v4

--- a/solution.py
+++ b/solution.py
@@ -299,19 +299,15 @@
         def _():
             y_second(0, i - PIECES // 2)
 
-            @pl.when(off == 0)
-            def _():
-                z_second(0, i - PIECES // 2)
-
     each(PIECES, early)
 
     def middle(i):
         arrived(r_piece(r_pair(1, 0) * 2 + c, i), x_recv.at[i])
         y_first(1, i)
 
-        @pl.when((i % 2) * (off % 2) == 1)
-        def _():
-            z_second(0, i // 2)
+        @pl.when((i // 4) * (1 - (off // 2) * (1 - off % 2)) == 1)
+        def _():
+            z_second(0, i - PIECES // 2)
 
         arrived(c_piece(own_b, i), b_recv.at[i])
         z_first(1, own_b, i)
@@ -339,6 +335,8 @@
     hand_over(1, up)
     hand_over(1, down)
     for half in range(PIECES // 2):
+        if half == 3:
+            y_last(1)
         z_second(1, half)
         if half == 0:
             y_last(0)
@@ -346,7 +344,6 @@
             flip, dy = ((1, up), (1, down), (0, 2))[half - 1]
             ready_rows(flip, dy)
             each(2, lambda slot: tile(r_pair(flip, dy), slot))
-    y_last(1)
     ready_columns(2)
     last = r_pair(1, 2)
     each(3, lambda m: block((last // 2 + 1 + m) % 4 * 2, 2, 2, blocks_of(2)))

time: 122 us -> 122 us (level)
  no operation moved by 1% of the time
where the time goes in v5:
time: 122 us
  Pallas kernels  122 us (100%)
    pallas_call x1, Pallas kernels, local(): pl.pallas_call(kernel, out_shape=pltpu.VMEM((16 * BLOCK, 8 * BLOCK), jnp....  119 us
    pallas_call x1, Pallas kernels, local(): pl.pallas_call(write_out, out_shape=jax.ShapeDtypeStruct(held.shape, held...  3.31 us

profile of v5, /device:TPU:35, one launch (start us, length us, event | category | flops | bytes accessed | tf_op | source)
XLA Modules:
  0.0 122.0 jit_solution(12108333647836676655)
XLA Ops:
  0.0 118.7 %shard_map.17.held = f32[2048,1024]{1,0:T(8,128)S(1)} custom-call(f32[64,32,128]{2,1,0:T(8,128)} %x_ref.1), custom_call_target="tpu_custom_call" | custom-call | tf_op jit(solution)/shard_map/pallas_call | solution.py:385
  118.7 3.3 %shard_map.18 = f32[2048,1024]{1,0:T(8,128)} custom-call(f32[2048,1024]{1,0:T(8,128)S(1)} %shard_map.17.held), custom_call_target="tpu_custom_call" | custom-call | tf_op jit(solution)/shard_map/pallas_call | solution.py:414
